TPU v7x, 32 devices: a whole 2x2x4 slice. The times are simulated.
32 devices in a mesh: row: 8 (over z, x), col: 4 (over y, core).
Axes of the slice: x: 2, y: 2, z: 4, core: 2. Of those that a mesh axis runs over, the one named last changes fastest.
Arguments:
- trailing: float32 [16384, 8192], P('row', 'col'), may hold values from -6 to 6
- vectors: float32 [16384, 256], P(('row', 'col')), may hold values from -0.1875 to 0.1875
- tfactor: float32 [256, 256], replicated, may hold values from -0.375 to 0.375
Outputs:
- updated: float32 [16384, 8192], P('row', 'col')
All inputs are finite; a program needn't handle non-finite values.
Results may differ from a plain program's by a relative error of at most 0.0003.
Values sent between devices are 32-bit elements.
A program may use at most 128 MiB of HBM per device.

v0:
```python
import jax
import jax.numpy as jnp
from jax import lax
from jax.sharding import PartitionSpec as P


def shards(trailing, vectors, tfactor):
    high = lax.Precision.HIGHEST
    near_vectors = lax.all_gather(vectors, "col", axis=0, tiled=True)
    partial_value = jnp.dot(
        near_vectors.T, trailing, precision=high, preferred_element_type=jnp.float32
    )
    summed = lax.psum(partial_value, "row")
    scaled = jnp.dot(tfactor, summed, precision=high, preferred_element_type=jnp.float32)
    change = jnp.dot(near_vectors, scaled, precision=high, preferred_element_type=jnp.float32)
    return trailing - change


def solution(mesh):
    placed = (P("row", "col"), P(("row", "col"), None), P())
    return jax.shard_map(
        shards, mesh=mesh, in_specs=placed, out_specs=P("row", "col"), check_vma=False
    )
```

profile of v0, /device:TPU:0, one launch (start us, length us, event | category | flops | bytes accessed | tf_op | source)
XLA Modules:
  0.0 203.2 jit_solution(18051398769543396435)
XLA Ops:
  6.5 0.0 copy-start
  6.5 0.0 all-gather.2.cloned.1.call-start
  6.5 0.7 all-gather.2.cloned.1.call-update
  7.3 0.0 all-reduce.2.cloned.1.call-start
  7.3 26.9 %all-gather.2.cloned.1.call-done = f32[2048,256]{1,0:T(8,128)} async-done(((f32[512,256]{1,0:T(8,128)}), f32[2048,256]{1,0:T(8,128)}) %all-gather.2.cloned.1.call-update) | async-done | bytes 2097168 | tf_op jit(solution)/shard_map/all_gather | solution.py:9
  34.2 18.3 %fusion = f32[256,2048]{1,0:T(8,128)} fusion(f32[2048,256]{1,0:T(8,128)} %all-gather.2.cloned.1.call-done, f32[2048,2048]{1,0:T(8,128)} %param.3), kind=kOutput, calls=%fused_computation.1 | convolution fusion | flops 12884901888 | bytes 20971520 | tf_op jit(solution)/shard_map/dot_general | solution.py:10
  52.5 0.0 all-reduce.2.cloned.1.call-update
  52.5 17.7 %copy.4 = f32[2048,2048]{0,1:T(8,128)} copy(f32[2048,2048]{1,0:T(8,128)} %param.3) | data formatting | bytes 33554432 | tf_op args[0]
  70.2 0.0 copy-start.2
  70.2 84.8 %all-reduce.2.cloned.1.call-done = f32[256,2048]{1,0:T(8,128)} async-done(((f32[256,2048]{1,0:T(8,128)}), f32[256,2048]{1,0:T(8,128)}) %all-reduce.2.cloned.1.call-update) | async-done | bytes 2097168 | tf_op jit(solution)/shard_map/psum | solution.py:13
  155.0 0.0 copy-done
  155.0 5.2 %fusion.1 = f32[2048,256]{1,0:T(8,128)S(1)} fusion(f32[256,2048]{1,0:T(8,128)} %all-reduce.2.cloned.1.call-done, f32[256,256]{1,0:T(8,128)S(1)} %copy-done), kind=kOutput, calls=%fused_computation.2 | convolution fusion | flops 1610612736 | bytes 4456448 | tf_op jit(solution)/shard_map/dot_general | solution.py:14
  160.2 0.0 copy-done.2
  160.2 18.5 %bitcast_subtract_fusion = f32[2048,2048]{0,1:T(8,128)} fusion(f32[2048,2048]{0,1:T(8,128)} %copy.4, f32[2048,256]{1,0:T(8,128)S(1)} %fusion.1, f32[2048,256]{1,0:T(8,128)S(1)} %copy-done.2), kind=kOutput, calls=%fused_computation | convolution fusion | flops 12889096192 | bytes 37748736 | tf_op jit(solution)/shard_map/dot_general | solution.py:15
  178.7 0.0 copy-start.1
  178.7 17.6 %copy.5 = f32[2048,2048]{1,0:T(8,128)} copy(f32[2048,2048]{0,1:T(8,128)} %bitcast_subtract_fusion) | data formatting | bytes 33554432 | tf_op jit(solution)/shard_map/sub | solution.py:16
  196.3 0.0 copy-done.1
Async XLA Ops:
  6.5 148.5 %copy-start = (f32[256,256]{1,0:T(8,128)S(1)}, f32[256,256]{1,0:T(8,128)}, u32[]{:S(2)}) copy-start(f32[256,256]{1,0:T(8,128)} %param.5) | copy-start | bytes 786436
  6.5 27.7 %all-gather.2.cloned.1.call-start = ((), (), s32[]{:S(2)}) async-start(), calls=%async_computation | async-start | bytes 2621440 | tf_op jit(solution)/shard_map/all_gather | solution.py:9
  7.3 147.7 %all-reduce.2.cloned.1.call-start = ((), (), s32[]{:S(2)}) async-start(), calls=%async_computation.1 | async-start | bytes 4194304 | tf_op jit(solution)/shard_map/psum | solution.py:13
  70.2 90.0 %copy-start.2 = (f32[2048,256]{1,0:T(8,128)S(1)}, f32[2048,256]{1,0:T(8,128)}, u32[]{:S(2)}) copy-start(f32[2048,256]{1,0:T(8,128)} %all-gather.2.cloned.1.call-done) | copy-start | bytes 6291460
  178.7 17.6 %copy-start.1 = (f32[256,256]{1,0:T(8,128)S(1)}, f32[256,256]{1,0:T(8,128)}, u32[]{:S(2)}) copy-start(f32[256,256]{1,0:T(8,128)} %param.5) | copy-start | bytes 786436
Sparse Core Ops, SparseCore 0:
  8.9 25.2 all-gather.1
  52.7 102.2 all-reduce.1
where the time goes:
time: 204 us; the launch traced here: 203 us
  waiting for transfers between devices  112 us (55%)
  matrix products  42 us (21%)
  local copies, waits for them, and re-layouts  35.3 us (17%)
  between operations  13.4 us (7%)
    psum x1, waiting for transfers between devices, shards(): summed = lax.psum(partial_value, 'row')  84.8 us
    all_gather x1, waiting for transfers between devices, shards(): near_vectors = lax.all_gather(vectors, 'col', axis=0, tiled=True)  26.9 us
    dot_general x1, matrix products, shards(): jnp.dot(near_vectors, scaled, precision=high, preferred_element_type=jnp....  18.5 us
    dot_general x1, matrix products, shards(): jnp.dot(near_vectors.T, trailing, precision=high, preferred_element_type=...  18.3 us
    unnamed x7, local copies, waits for them, and re-layouts  17.7 us
    sub x1, local copies, waits for them, and re-layouts, shards(): return trailing - change  17.6 us
    dot_general x1, matrix products, shards(): jnp.dot(tfactor, summed, precision=high, preferred_element_type=jnp.float32)  5.17 us
  transfers between devices with their start and end apart: 2, of which 2 were waited for; matrix products, arithmetic and copies ran while one was open for 9% of the time, Pallas kernels for 0%

commit v1 on v0

--- a/solution.py
+++ b/solution.py
@@ -10,7 +10,10 @@
     partial_value = jnp.dot(
         near_vectors.T, trailing, precision=high, preferred_element_type=jnp.float32
     )
-    summed = lax.psum(partial_value, "row")
+    _process_weights = lambda device_axis, local_array: jnp.sum(
+        jax.lax.all_gather(local_array, device_axis), axis=0
+    )
+    summed = _process_weights("row", local_array=partial_value)
     scaled = jnp.dot(tfactor, summed, precision=high, preferred_element_type=jnp.float32)
     change = jnp.dot(near_vectors, scaled, precision=high, preferred_element_type=jnp.float32)
     return trailing - change

time: 204 us -> 335 us (1.64)
  waiting for transfers between devices: 112 us -> 237 us
  other arithmetic: 0 us -> 7.76 us
    all_gather x0 -> x1, waiting for transfers between devices: none -> 209 us  [shards(): jax.lax.all_gather(local_array, device_axis)]
    psum x1 -> x0, waiting for transfers between devices: 84.8 us -> none  [shards(): summed = lax.psum(partial_value, 'row')]
    reduce_sum x0 -> x1, other arithmetic: none -> 7.76 us  [shards(): jnp.sum(jax.lax.all_gather(local_array, device_axis), axis=0)]
  transfers between devices with their start and end apart: 2 -> 2, of which waited for: 2 -> 2; matrix products, arithmetic and copies ran while one was open for 9% -> 5% of each run, Pallas kernels for 0% -> 0%
where the time goes in v1:
time: 335 us; the launch traced here: 334 us
  waiting for transfers between devices  237 us (71%)
  matrix products  40.5 us (12%)
  local copies, waits for them, and re-layouts  35.6 us (11%)
  between operations  13.4 us (4%)
  other arithmetic  7.76 us (2%)
    all_gather x1, waiting for transfers between devices, shards(): jax.lax.all_gather(local_array, device_axis)  209 us
    all_gather x1, waiting for transfers between devices, shards(): near_vectors = lax.all_gather(vectors, 'col', axis=0, tiled=True)  26.9 us
    dot_general x1, matrix products, shards(): jnp.dot(near_vectors, scaled, precision=high, preferred_element_type=jnp....  18.7 us
    dot_general x1, matrix products, shards(): jnp.dot(near_vectors.T, trailing, precision=high, preferred_element_type=...  18.3 us
    unnamed x7, local copies, waits for them, and re-layouts  18 us
    sub x1, local copies, waits for them, and re-layouts, shards(): return trailing - change  17.6 us
    reduce_sum x1, other arithmetic, shards(): jnp.sum(jax.lax.all_gather(local_array, device_axis), axis=0)  7.76 us
  transfers between devices with their start and end apart: 2, of which 2 were waited for; matrix products, arithmetic and copies ran while one was open for 5% of the time, Pallas kernels for 0%

profile of v1, /device:TPU:0, one launch (start us, length us, event | category | flops | bytes accessed | tf_op | source)
XLA Modules:
  0.0 334.5 jit_solution(3366589063080867662)
XLA Ops:
  6.5 0.0 copy-start
  6.5 0.0 all-gather.4.cloned.1.call-start
  6.5 0.7 all-gather.4.cloned.1.call-update
  7.3 0.0 all-gather.6.cloned.1.call-start
  7.3 26.9 %all-gather.4.cloned.1.call-done = f32[2048,256]{1,0:T(8,128)} async-done(((f32[512,256]{1,0:T(8,128)}), f32[2048,256]{1,0:T(8,128)}) %all-gather.4.cloned.1.call-update) | async-done | bytes 2097168 | tf_op jit(solution)/shard_map/all_gather | solution.py:9
  34.2 18.3 %fusion = f32[256,2048]{1,0:T(8,128)} fusion(f32[2048,256]{1,0:T(8,128)} %all-gather.4.cloned.1.call-done, f32[2048,2048]{1,0:T(8,128)} %param.3), kind=kOutput, calls=%fused_computation.1 | convolution fusion | flops 12884901888 | bytes 20971520 | tf_op jit(solution)/shard_map/dot_general | solution.py:10
  52.5 0.0 all-gather.6.cloned.1.call-update
  52.6 18.0 %copy.4 = f32[2048,2048]{0,1:T(8,128)} copy(f32[2048,2048]{1,0:T(8,128)} %param.3) | data formatting | bytes 33554432 | tf_op args[0]
  70.5 209.5 %all-gather.6.cloned.1.call-done = f32[2048,2048]{1,0:T(8,128)} async-done(((f32[256,2048]{1,0:T(8,128)}), f32[2048,2048]{1,0:T(8,128)}) %all-gather.6.cloned.1.call-update) | async-done | bytes 16777232 | tf_op jit(solution)/shard_map/all_gather | solution.py:14
  280.0 7.8 %reduce_sum.9 = f32[256,2048]{1,0:T(8,128)S(1)} reduce(f32[8,256,2048]{2,1,0:T(8,128)} %bitcast.9, f32[]{:T(128)} %constant.0.clone.1), dimensions={0}, to_apply=%region_0.0 | reduce | flops 3670016 | bytes 18874372 | tf_op jit(solution)/shard_map/reduce_sum | solution.py:13
  287.8 0.0 copy-done
  287.8 0.0 copy-start.2
  287.8 3.5 %fusion.1 = f32[2048,256]{1,0:T(8,128)S(1)} fusion(f32[256,2048]{1,0:T(8,128)S(1)} %reduce_sum.9, f32[256,256]{1,0:T(8,128)S(1)} %copy-done), kind=kOutput, calls=%fused_computation.2 | convolution fusion | flops 1610612736 | bytes 4456448 | tf_op jit(solution)/shard_map/dot_general | solution.py:17
  291.3 0.0 copy-done.2
  291.3 18.7 %bitcast_subtract_fusion = f32[2048,2048]{0,1:T(8,128)} fusion(f32[2048,2048]{0,1:T(8,128)} %copy.4, f32[2048,256]{1,0:T(8,128)S(1)} %fusion.1, f32[2048,256]{1,0:T(8,128)S(1)} %copy-done.2), kind=kOutput, calls=%fused_computation | convolution fusion | flops 12889096192 | bytes 37748736 | tf_op jit(solution)/shard_map/dot_general | solution.py:18
  310.0 0.0 copy-start.1
  310.0 17.6 %copy.5 = f32[2048,2048]{1,0:T(8,128)} copy(f32[2048,2048]{0,1:T(8,128)} %bitcast_subtract_fusion) | data formatting | bytes 33554432 | tf_op jit(solution)/shard_map/sub | solution.py:19
  327.6 0.0 copy-done.1
Async XLA Ops:
  6.5 281.2 %copy-start = (f32[256,256]{1,0:T(8,128)S(1)}, f32[256,256]{1,0:T(8,128)}, u32[]{:S(2)}) copy-start(f32[256,256]{1,0:T(8,128)} %param.5) | copy-start | bytes 786436
  6.5 27.7 %all-gather.4.cloned.1.call-start = ((), (), s32[]{:S(2)}) async-start(), calls=%async_computation | async-start | bytes 2621440 | tf_op jit(solution)/shard_map/all_gather | solution.py:9
  7.3 272.7 %all-gather.6.cloned.1.call-start = ((), (), s32[]{:S(2)}) async-start(), calls=%async_computation.1 | async-start | bytes 18874368 | tf_op jit(solution)/shard_map/all_gather | solution.py:14
  287.8 3.5 %copy-start.2 = (f32[2048,256]{1,0:T(8,128)S(1)}, f32[2048,256]{1,0:T(8,128)}, u32[]{:S(2)}) copy-start(f32[2048,256]{1,0:T(8,128)} %all-gather.4.cloned.1.call-done) | copy-start | bytes 6291460
  310.0 17.6 %copy-start.1 = (f32[256,256]{1,0:T(8,128)S(1)}, f32[256,256]{1,0:T(8,128)}, u32[]{:S(2)}) copy-start(f32[256,256]{1,0:T(8,128)} %param.5) | copy-start | bytes 786436
Sparse Core Ops, SparseCore 0:
  8.9 25.2 all-gather.3
  52.7 227.2 all-gather.5

commit v2 on v0

--- a/solution.py
+++ b/solution.py
@@ -6,7 +6,13 @@
 
 def shards(trailing, vectors, tfactor):
     high = lax.Precision.HIGHEST
-    near_vectors = lax.all_gather(vectors, "col", axis=0, tiled=True)
+    n_dev = lax.axis_size("col")
+    held, blocks = (vectors, [vectors])
+    for _ in range(n_dev - 1):
+        held = lax.ppermute(held, "col", [(i, (i + 1) % n_dev) for i in range(n_dev)])
+        blocks.insert(0, held)
+    row_of_blocks = jnp.concatenate(blocks, axis=0)
+    near_vectors = jnp.roll(row_of_blocks, (lax.axis_index("col") + 1) * vectors.shape[0], axis=0)
     partial_value = jnp.dot(
         near_vectors.T, trailing, precision=high, preferred_element_type=jnp.float32
     )

time: 204 us -> 190 us (0.931)
  local copies, waits for them, and re-layouts: 35.3 us -> 3.35 us
  waiting for transfers between devices: 112 us -> 131 us
    all_gather x1 -> x0, waiting for transfers between devices: 26.9 us -> none  [shards(): near_vectors = lax.all_gather(vectors, 'col', axis=0, tiled=True)]
    ppermute x0 -> x3, waiting for transfers between devices: none -> 26.2 us  [shards(): lax.ppermute(held, 'col', [(i, (i + 1) % n_dev) for i in range(n_dev)])]
    psum x1, waiting for transfers between devices: 84.8 us -> 104 us  [shards(): summed = lax.psum(partial_value, 'row')]
    sub x1 -> x0, local copies, waits for them, and re-layouts: 17.6 us -> none  [shards(): return trailing - change]
    unnamed x7 -> x15, local copies, waits for them, and re-layouts: 17.7 us -> 3.32 us
  transfers between devices with their start and end apart: 2 -> 4, of which waited for: 2 -> 4; matrix products, arithmetic and copies ran while one was open for 9% -> 0% of each run, Pallas kernels for 0% -> 0%
where the time goes in v2:
time: 190 us
  waiting for transfers between devices  131 us (69%)
  matrix products  41.5 us (22%)
  between operations  13.5 us (7%)
  local copies, waits for them, and re-layouts  3.35 us (2%)
    psum x1, waiting for transfers between devices, shards(): summed = lax.psum(partial_value, 'row')  104 us
    ppermute x3, waiting for transfers between devices, shards(): lax.ppermute(held, 'col', [(i, (i + 1) % n_dev) for i in range(n_dev)])  26.2 us
    dot_general x1, matrix products, shards(): jnp.dot(near_vectors, scaled, precision=high, preferred_element_type=jnp....  18.5 us
    dot_general x1, matrix products, shards(): jnp.dot(near_vectors.T, trailing, precision=high, preferred_element_type=...  17.7 us
    dot_general x1, matrix products, shards(): jnp.dot(tfactor, summed, precision=high, preferred_element_type=jnp.float32)  5.32 us
  transfers between devices with their start and end apart: 4, of which 4 were waited for; matrix products, arithmetic and copies ran while one was open for 0% of the time, Pallas kernels for 0%

profile of v2, /device:TPU:0, one launch (start us, length us, event | category | flops | bytes accessed | tf_op | source)
XLA Modules:
  0.0 189.6 jit_solution(16563419707419132213)
XLA Ops:
  6.5 0.0 copy-start
  6.5 0.0 copy-start.3
  6.5 0.0 all-reduce.2.cloned.1.call-start
  6.5 0.5 collective-permute-start
  7.0 9.0 %collective-permute-done = f32[512,256]{1,0:T(8,128)S(1)} collective-permute-done((f32[512,256]{1,0:T(8,128)}, f32[512,256]{1,0:T(8,128)S(1)}, u32[]{:S(2)}, u32[]{:S(2)}) %collective-permute-start) | collective-permute-done | bytes 524320 | tf_op jit(solution)/shard_map/ppermute | solution.py:12
  16.1 0.0 collective-permute-start.1
  16.1 8.6 %collective-permute-done.1 = f32[512,256]{1,0:T(8,128)S(1)} collective-permute-done((f32[512,256]{1,0:T(8,128)S(1)}, f32[512,256]{1,0:T(8,128)S(1)}, u32[]{:S(2)}, u32[]{:S(2)}) %collective-permute-start.1) | collective-permute-done | bytes 524320 | tf_op jit(solution)/shard_map/ppermute | solution.py:12
  24.7 0.0 collective-permute-start.2
  24.7 8.6 %collective-permute-done.2 = f32[512,256]{1,0:T(8,128)S(1)} collective-permute-done((f32[512,256]{1,0:T(8,128)S(1)}, f32[512,256]{1,0:T(8,128)S(1)}, u32[]{:S(2)}, u32[]{:S(2)}) %collective-permute-start.2) | collective-permute-done | bytes 524320 | tf_op jit(solution)/shard_map/ppermute | solution.py:12
  33.4 1.1 constant_dynamic-update-slice_fusion.4
  34.6 0.0 copy-done.3
  34.7 0.0 copy-start.1
  34.7 2.0 %copy-done.1 = f32[4096,256]{1,0:T(8,128)} copy-done((f32[4096,256]{1,0:T(8,128)}, f32[4096,256]{1,0:T(8,128)S(1)}, u32[]{:S(2)}) %copy-start.1) | copy-done | bytes 4194328
  36.7 17.7 %fusion.1 = f32[256,2048]{1,0:T(8,128)} fusion(f32[2048,2048]{1,0:T(8,128)} %param.3, f32[4096,256]{1,0:T(8,128)S(1)} %constant_dynamic-update-slice_fusion, s32[]{:T(128)S(6)} %select_n.14), kind=kOutput, calls=%fused_computation.2 | convolution fusion | flops 12884901888 | bytes 20971524 | tf_op jit(solution)/shard_map/dot_general | solution.py:16
  54.4 0.0 all-reduce.2.cloned.1.call-update
  54.4 104.5 %all-reduce.2.cloned.1.call-done = f32[256,2048]{1,0:T(8,128)} async-done(((f32[256,2048]{1,0:T(8,128)}), f32[256,2048]{1,0:T(8,128)}) %all-reduce.2.cloned.1.call-update) | async-done | bytes 2097168 | tf_op jit(solution)/shard_map/psum | solution.py:19
  158.9 0.0 copy-done
  158.9 0.0 copy-start.2
  158.9 5.3 %fusion.5 = f32[2048,256]{1,0:T(8,128)S(1)} fusion(f32[256,2048]{1,0:T(8,128)} %all-reduce.2.cloned.1.call-done, f32[256,256]{1,0:T(8,128)S(1)} %copy-done), kind=kOutput, calls=%fused_computation.14 | convolution fusion | flops 1610612736 | bytes 4456448 | tf_op jit(solution)/shard_map/dot_general | solution.py:20
  164.2 0.0 copy-done.2
  164.3 18.5 %convolution_subtract_fusion = f32[2048,2048]{1,0:T(8,128)} fusion(f32[2048,2048]{1,0:T(8,128)} %param.3, f32[2048,256]{1,0:T(8,128)S(1)} %fusion.5, f32[4096,256]{1,0:T(8,128)S(1)} %copy-done.2, s32[]{:T(128)S(6)} %select_n.14), kind=kOutput, calls=%fused_computation | convolution fusion | flops 12889096192 | bytes 37748740 | tf_op jit(solution)/shard_map/dot_general | solution.py:21
  (7 shorter events, 0.3 us)
Async XLA Ops:
  6.5 152.4 %copy-start = (f32[256,256]{1,0:T(8,128)S(1)}, f32[256,256]{1,0:T(8,128)}, u32[]{:S(2)}) copy-start(f32[256,256]{1,0:T(8,128)} %param.5) | copy-start | bytes 786436
  6.5 28.1 %copy-start.3 = (f32[512,256]{1,0:T(8,128)S(1)}, f32[512,256]{1,0:T(8,128)}, u32[]{:S(2)}) copy-start(f32[512,256]{1,0:T(8,128)} %param.4) | copy-start | bytes 1572868
  6.5 152.4 %all-reduce.2.cloned.1.call-start = ((), (), s32[]{:S(2)}) async-start(), calls=%async_computation | async-start | bytes 4194304 | tf_op jit(solution)/shard_map/psum | solution.py:19
  6.5 9.5 %collective-permute-start = (f32[512,256]{1,0:T(8,128)}, f32[512,256]{1,0:T(8,128)S(1)}, u32[]{:S(2)}, u32[]{:S(2)}) collective-permute-start(f32[512,256]{1,0:T(8,128)} %param.4), channel_id=1, source_target_pairs={{0,1},{1,2},{2,3},{3,0},{4,5},{5,6},{6,7},{7,4},{8,9},{9,10},{10,1... | collective-permute-start | bytes 1572872 | tf_op jit(solution)/shard_map/ppermute | solution.py:12
  16.1 8.6 %collective-permute-start.1 = (f32[512,256]{1,0:T(8,128)S(1)}, f32[512,256]{1,0:T(8,128)S(1)}, u32[]{:S(2)}, u32[]{:S(2)}) collective-permute-start(f32[512,256]{1,0:T(8,128)S(1)} %collective-permute-done), channel_id=1, source_target_pairs={{0,1},{1,2},{2,3},{3,0},{4,5},{5,6},{6,7},{7,4},{8,9},{9,10},{10,1... | collective-permute-start | bytes 1572872 | tf_op jit(solution)/shard_map/ppermute | solution.py:12
  24.7 8.6 %collective-permute-start.2 = (f32[512,256]{1,0:T(8,128)S(1)}, f32[512,256]{1,0:T(8,128)S(1)}, u32[]{:S(2)}, u32[]{:S(2)}) collective-permute-start(f32[512,256]{1,0:T(8,128)S(1)} %collective-permute-done.1), channel_id=1, source_target_pairs={{0,1},{1,2},{2,3},{3,0},{4,5},{5,6},{6,7},{7,4},{8,9},{9,10},{10,1... | collective-permute-start | bytes 1572872 | tf_op jit(solution)/shard_map/ppermute | solution.py:12
  34.7 2.0 %copy-start.1 = (f32[4096,256]{1,0:T(8,128)}, f32[4096,256]{1,0:T(8,128)S(1)}, u32[]{:S(2)}) copy-start(f32[4096,256]{1,0:T(8,128)S(1)} %constant_dynamic-update-slice_fusion) | copy-start | bytes 12582916
  158.9 5.3 %copy-start.2 = (f32[4096,256]{1,0:T(8,128)S(1)}, f32[4096,256]{1,0:T(8,128)}, u32[]{:S(2)}) copy-start(f32[4096,256]{1,0:T(8,128)} %copy-done.1) | copy-start | bytes 12582916
Sparse Core Ops, SparseCore 0:
  54.6 104.3 all-reduce.1
